TPU v7x, 32 devices: a whole 2x2x4 slice. The times are simulated.
32 devices in a mesh: grp: 2 (over x), freq: 16 (over z, y, core).
Axes of the slice: x: 2, y: 2, z: 4, core: 2. Of those that a mesh axis runs over, the one named last changes fastest.
Arguments:
- kernel: bfloat16 [2, 256, 1024, 1024], P(None, ('grp', 'freq')), parts along dimension 1, may hold values from -0.125 to 0.125
- recorded: float32 [2, 256, 1024, 128], P(None, ('grp', 'freq')), parts along dimension 1, may hold values from -8 to 8
- onset_time: int32 [2048, 128], P(('grp', 'freq')), parts along dimension 0, may hold values from 32 to 256, as said below
Outputs:
- focusing: float32 [256, 2048, 128], P(None, ('grp', 'freq')), parts along dimension 1
There are 2 independent parts, one for each index of `grp`. A program takes and returns all parts, laid end to end along the dimension named above; each array names one. Nothing has to cross between parts.
Inputs may be any that keep to these rules, and one draw needn't show every extreme that they name: `onset_time`: onset sample of the window for each receiver and focal point.
All inputs are finite; a program needn't handle non-finite values.
Results may differ from a plain program's by a relative error of at most 0.012.
Values may be sent and summed in bfloat16 or wider, within the bound.
A program may use at most 192 MiB of HBM per device.

v0:
```python
import math
import jax
import jax.numpy as jnp
from jax import lax
from jax.sharding import PartitionSpec as P

NF = 128
ITERS = 2


def dft_tables():
    samples = jnp.arange(2 * NF, dtype=jnp.int32)
    bins = jnp.arange(NF, dtype=jnp.int32)
    phase = (bins[:, None] * samples[None, :] % (2 * NF)).astype(jnp.float32) * (math.pi / NF)
    factor = 1.0 / math.sqrt(NF)
    return (jnp.cos(phase) * factor, jnp.sin(phase) * factor)


def square_sum(values):
    return jnp.sum(values * values)


def joint_total(first, second, third):
    return lax.psum((first, second, third), "freq")


def body(kernel, recorded, onset_time):
    highest = lax.Precision.HIGHEST
    cosine_table, sin_tab = dft_tables()
    rec_local = onset_time.shape[0]
    focal_count = onset_time.shape[1]
    samples = lax.broadcasted_iota(jnp.int32, (2 * NF, rec_local, focal_count), 0)
    keep_mask = (samples < onset_time[None]).astype(jnp.float32)
    kernel_real = kernel[0]
    kernel_imaginary = kernel[1]

    def invert(block_in):
        columns = block_in.shape[3]
        widened = block_in.astype(jnp.float32)
        timed = jnp.dot(cosine_table.T, widened[0].reshape(NF, -1), precision=highest) - jnp.dot(
            sin_tab.T, widened[1].reshape(NF, -1), precision=highest
        )
        return timed.reshape(2 * NF, block_in.shape[2], columns)

    def apply_adjoint(resid):
        rounded = resid.astype(jnp.bfloat16)
        update_real = rounded[0]
        update_imaginary = rounded[1]
        z_real = jnp.einsum(
            "hvi,hvg->hig", kernel_real, update_real, preferred_element_type=jnp.float32
        ) + jnp.einsum(
            "hvi,hvg->hig", kernel_imaginary, update_imaginary, preferred_element_type=jnp.float32
        )
        z_imag = jnp.einsum(
            "hvi,hvg->hig", kernel_real, update_imaginary, preferred_element_type=jnp.float32
        ) - jnp.einsum(
            "hvi,hvg->hig", kernel_imaginary, update_real, preferred_element_type=jnp.float32
        )
        image = jnp.stack([z_real, z_imag]).astype(jnp.bfloat16)
        timed = invert(lax.all_to_all(image, "freq", split_axis=2, concat_axis=1, tiled=True))
        return timed * keep_mask

    model_raw = apply_adjoint(recorded)
    totals = joint_total(square_sum(recorded), square_sum(model_raw), jnp.float32(0.0))
    beta_now = jnp.sqrt(totals[0])
    data_vec = recorded / beta_now
    alpha_now = jnp.sqrt(totals[1]) / beta_now
    model_vec = model_raw / (alpha_now * beta_now)
    search = model_vec
    estimate = jnp.zeros_like(model_vec)
    phibar_now = beta_now
    rhobar_now = alpha_now
    for iteration in range(ITERS):
        flat_part = (model_vec * keep_mask).reshape(2 * NF, -1)
        spec_real = jnp.dot(cosine_table, flat_part, precision=highest)
        spec_imag = -jnp.dot(sin_tab, flat_part, precision=highest)
        spectrum = (
            jnp.stack([spec_real, spec_imag])
            .reshape(2, NF, rec_local, focal_count)
            .astype(jnp.bfloat16)
        )
        multiply_block_in = lax.all_to_all(
            spectrum, "freq", split_axis=1, concat_axis=2, tiled=True
        )
        solution_real = multiply_block_in[0]
        solution_imaginary = multiply_block_in[1]
        y_real = jnp.einsum(
            "ptx,pxi->pti", kernel_real, solution_real, preferred_element_type=jnp.float32
        ) - jnp.einsum(
            "ptx,pxi->pti", kernel_imaginary, solution_imaginary, preferred_element_type=jnp.float32
        )
        y_imag = jnp.einsum(
            "ptx,pxi->pti", kernel_real, solution_imaginary, preferred_element_type=jnp.float32
        ) + jnp.einsum(
            "ptx,pxi->pti", kernel_imaginary, solution_real, preferred_element_type=jnp.float32
        )
        data_raw = jnp.stack([y_real, y_imag]) - alpha_now * data_vec
        image_raw = apply_adjoint(data_raw)
        totals = joint_total(
            square_sum(data_raw), square_sum(image_raw), jnp.sum(image_raw * model_vec)
        )
        beta_now = jnp.sqrt(totals[0])
        data_vec = data_raw / beta_now
        alpha_now = jnp.sqrt(
            totals[1] / (beta_now * beta_now) - 2.0 * totals[2] + beta_now * beta_now
        )
        model_vec = (image_raw / beta_now - beta_now * model_vec) / alpha_now
        rho_now = jnp.sqrt(rhobar_now * rhobar_now + beta_now * beta_now)
        cosine = rhobar_now / rho_now
        sine_part = beta_now / rho_now
        theta_now = sine_part * alpha_now
        rhobar_now = -cosine * alpha_now
        phi_now = cosine * phibar_now
        phibar_now = sine_part * phibar_now
        estimate = estimate + phi_now / rho_now * search
        search = model_vec - theta_now / rho_now * search
    return estimate


def solution(mesh):
    placed = (
        P(None, ("grp", "freq"), None, None),
        P(None, ("grp", "freq"), None, None),
        P(("grp", "freq"), None),
    )
    return jax.shard_map(
        body, mesh=mesh, in_specs=placed, out_specs=P(None, ("grp", "freq"), None), check_vma=False
    )
```

profile of v0, /device:TPU:0, one launch (start us, length us, event | category | flops | bytes accessed | tf_op | source)
XLA Modules:
  0.0 832.4 jit_solution(1631037788863570241)
XLA Ops:
  0.0 8.5 %multiply_reduce_fusion.3 = (f32[]{:T(128)}, bf16[2,8,1024,128]{3,2,1,0:T(8,128)(2,1)S(1)}) fusion(f32[2,8,1024,128]{3,2,1,0:T(8,128)} %param.4), kind=kLoop, calls=%fused_computation.57 | loop fusion | flops 6291455 | bytes 12582916 | tf_op jit(solution)/shard_map/reduce_sum | solution.py:20
  8.5 10.8 %fusion.14 = f32[8,1024,128]{2,1,0:T(8,128)} fusion(bf16[2,8,1024,1024]{3,2,1,0:T(8,128)(2,1)} %param.3, bf16[2,8,1024,128]{3,2,1,0:T(8,128)(2,1)S(1)} %get-tuple-element.15), kind=kOutput, calls=%fused_computation.14 | convolution fusion | flops 2147483648 | bytes 23068672 | tf_op jit(solution)/shard_map/hvi,hvg->hig/dot_general | solution.py:51
  19.4 10.7 %fusion.12 = f32[8,1024,128]{2,1,0:T(8,128)} fusion(bf16[2,8,1024,1024]{3,2,1,0:T(8,128)(2,1)} %param.3, bf16[2,8,1024,128]{3,2,1,0:T(8,128)(2,1)S(1)} %get-tuple-element.15), kind=kOutput, calls=%fused_computation.12 | convolution fusion | flops 2147483648 | bytes 23068672 | tf_op jit(solution)/shard_map/hvi,hvg->hig/dot_general | solution.py:56
  30.0 9.6 %fusion.67 = bf16[1,8,1024,128]{3,2,1,0:T(8,128)(2,1)S(1)} fusion(f32[8,1024,128]{2,1,0:T(8,128)} %fusion.14, bf16[2,8,1024,128]{3,2,1,0:T(8,128)(2,1)S(1)} %get-tuple-element.15, bf16[2,8,1024,1024]{3,2,1,0:T(8,128)(2,1)} %param.3), kind=kOutput, calls=%fused_computation.97 | convolution fusion | flops 2149580800 | bytes 25165824 | tf_op jit(solution)/shard_map/hvi,hvg->hig/dot_general | solution.py:49
  39.7 10.4 %fusion.68 = bf16[1,8,1024,128]{3,2,1,0:T(8,128)(2,1)S(1)} fusion(f32[8,1024,128]{2,1,0:T(8,128)} %fusion.12, bf16[2,8,1024,128]{3,2,1,0:T(8,128)(2,1)S(1)} %get-tuple-element.15, bf16[2,8,1024,1024]{3,2,1,0:T(8,128)(2,1)} %param.3), kind=kOutput, calls=%fused_computation.98 | convolution fusion | flops 2149580800 | bytes 25165824 | tf_op jit(solution)/shard_map/hvi,hvg->hig/dot_general | solution.py:54
  50.5 2.7 copy.81
  53.2 99.3 %all_to_all.60 = bf16[2,8,1024,128]{3,1,0,2:T(8,128)(2,1)S(1)} all-to-all(bf16[2,8,1024,128]{3,1,0,2:T(8,128)(2,1)S(1)} %copy.81), channel_id=1, replica_groups=mesh['grp'=2,'freq'=16] {'freq'}, dimensions={2} | all-to-all | bytes 8388608 | tf_op jit(solution)/shard_map/all_to_all | solution.py:60
  154.6 4.4 fusion.78
  159.0 12.1 %multiply_reduce_fusion.4 = (f32[]{:T(128)}, f32[256,8192]{1,0:T(8,128)}) fusion(s32[8192]{0:T(1024)S(1)} %bitcast.250, f32[256,8192]{1,0:T(8,128)S(1)} %fusion.78, bf16[16,8,64,128]{3,2,1,0:T(8,128)(2,1)S(1)} %get-tuple-element.22), kind=kOutput, calls=%fused_computation.58 | convolution fusion | flops 3232202752 | bytes 18907140 | tf_op jit(solution)/shard_map/dot_general | solution.py:40
  171.1 34.1 %all-reduce.1 = (f32[]{:T(128)}, f32[]{:T(128)}) all-reduce(f32[]{:T(128)} %get-tuple-element.24, f32[]{:T(128)} %get-tuple-element.14), channel_id=1, replica_groups=mesh['grp'=2,'freq'=16] {'freq'}, use_global_device_ids=true, to_apply=%region_1.2 | all-reduce | flops 2 | bytes 16 | tf_op jit(solution)/shard_map/psum | solution.py:24
  206.5 10.7 %fusion.89 = bf16[16,8,64,128]{3,1,2,0:T(8,128)(2,1)S(1)} fusion(s32[8192]{0:T(1024)S(1)} %bitcast.251, f32[256,8192]{1,0:T(8,128)} %get-tuple-element.25, f32[]{:T(128)S(6)} %mul.210), kind=kOutput, calls=%fused_computation.123 | convolution fusion | flops 3231154176 | bytes 10518532 | tf_op jit(solution)/shard_map/dot_general | solution.py:75
  217.2 7.5 fusion.94
  226.9 2.3 pad_maximum_fusion.1
  229.2 4.5 all-to-all-start.1
  233.8 8.7 %copy.96 = f32[2,8,1024,128]{2,3,1,0:T(8,128)} copy(f32[2,8,1024,128]{3,2,1,0:T(8,128)} %param.4) | data formatting | bytes 16777216 | tf_op args[1]
  242.5 68.8 %all-to-all-done.1 = bf16[2,128,64,128]{3,2,0,1:T(8,128)(2,1)} async-done(((bf16[2,128,64,128]{3,2,0,1:T(8,128)(2,1)}), bf16[2,128,64,128]{3,2,0,1:T(8,128)(2,1)}, u32[]{:S(2)}, u32[]{:S(2)}) %all-to-all-start.1) | async-done | bytes 4194336 | tf_op jit(solution)/shard_map/all_to_all | solution.py:82
  311.2 3.1 copy.85
  316.9 14.0 %fusion.10 = f32[8,128,1024]{2,1,0:T(8,128)} fusion(bf16[8,1024,128]{2,1,0:T(8,128)(2,1)} %bitcast.241, bf16[2,8,1024,1024]{3,2,1,0:T(8,128)(2,1)} %param.3), kind=kOutput, calls=%fused_computation.10 | convolution fusion | flops 2147483648 | bytes 23068672 | tf_op jit(solution)/shard_map/ptx,pxi->pti/dot_general | solution.py:89
  332.5 14.0 %fusion.8 = f32[8,128,1024]{2,1,0:T(8,128)} fusion(bf16[8,1024,128]{2,1,0:T(8,128)(2,1)} %bitcast.246, bf16[2,8,1024,1024]{3,2,1,0:T(8,128)(2,1)} %param.3), kind=kOutput, calls=%fused_computation.8 | convolution fusion | flops 2147483648 | bytes 23068672 | tf_op jit(solution)/shard_map/ptx,pxi->pti/dot_general | solution.py:94
  346.5 10.8 %subtract_bitcast_fusion.1 = f32[1,8,1024,128]{2,3,1,0:T(8,128)S(1)} fusion(f32[8,128,1024]{2,1,0:T(8,128)} %fusion.10, bf16[8,1024,128]{2,1,0:T(8,128)(2,1)} %bitcast.247, bf16[2,8,1024,1024]{3,2,1,0:T(8,128)(2,1)} %param.3), kind=kOutput, calls=%fused_computation.74 | convolution fusion | flops 2148532224 | bytes 27262976 | tf_op jit(solution)/shard_map/ptx,pxi->pti/dot_general | solution.py:87
  357.3 11.2 %add_bitcast_fusion.1 = f32[1,8,1024,128]{2,3,1,0:T(8,128)} fusion(f32[8,128,1024]{2,1,0:T(8,128)} %fusion.8, bf16[8,1024,128]{2,1,0:T(8,128)(2,1)S(1)} %bitcast.242, bf16[2,8,1024,1024]{3,2,1,0:T(8,128)(2,1)} %param.3), kind=kOutput, calls=%fused_computation.73 | convolution fusion | flops 2148532224 | bytes 27262976 | tf_op jit(solution)/shard_map/ptx,pxi->pti/dot_general | solution.py:92
  368.5 6.4 multiply_reduce_fusion.2
  374.9 3.2 copy-done.1
  378.8 10.1 %fusion.6 = f32[8,128,1024]{2,1,0:T(8,128)} fusion(bf16[2,8,1024,1024]{3,2,1,0:T(8,128)(2,1)} %param.3, bf16[2,8,1024,128]{2,3,1,0:T(8,128)(2,1)S(1)} %convert_element_type.32), kind=kOutput, calls=%fused_computation.6 | convolution fusion | flops 2147483648 | bytes 23068672 | tf_op jit(solution)/shard_map/hvi,hvg->hig/dot_general | solution.py:51
  388.9 10.1 %fusion.4 = f32[8,128,1024]{2,1,0:T(8,128)} fusion(bf16[2,8,1024,1024]{3,2,1,0:T(8,128)(2,1)} %param.3, bf16[2,8,1024,128]{2,3,1,0:T(8,128)(2,1)S(1)} %convert_element_type.32), kind=kOutput, calls=%fused_computation.4 | convolution fusion | flops 2147483648 | bytes 23068672 | tf_op jit(solution)/shard_map/hvi,hvg->hig/dot_general | solution.py:56
  399.0 9.4 %fusion.69 = bf16[1,8,1024,128]{2,3,1,0:T(8,128)(2,1)S(1)} fusion(f32[8,128,1024]{2,1,0:T(8,128)} %fusion.6, bf16[2,8,1024,1024]{3,2,1,0:T(8,128)(2,1)} %param.3, bf16[2,8,1024,128]{2,3,1,0:T(8,128)(2,1)S(1)} %convert_element_type.32), kind=kOutput, calls=%fused_computation.99 | convolution fusion | flops 2149580800 | bytes 25165824 | tf_op jit(solution)/shard_map/hvi,hvg->hig/dot_general | solution.py:49
  408.5 10.8 %fusion.70 = bf16[1,8,1024,128]{2,3,1,0:T(8,128)(2,1)} fusion(f32[8,128,1024]{2,1,0:T(8,128)} %fusion.4, bf16[2,8,1024,1024]{3,2,1,0:T(8,128)(2,1)} %param.3, bf16[2,8,1024,128]{2,3,1,0:T(8,128)(2,1)S(1)} %convert_element_type.32), kind=kOutput, calls=%fused_computation.100 | convolution fusion | flops 2149580800 | bytes 25165824 | tf_op jit(solution)/shard_map/hvi,hvg->hig/dot_general | solution.py:54
  419.3 3.9 pad_maximum_fusion.2
  423.2 6.9 copy.101
  430.2 112.1 %all_to_all.61 = bf16[2,8,1024,128]{3,1,0,2:T(8,128)(2,1)S(1)} all-to-all(bf16[2,8,1024,128]{3,1,0,2:T(8,128)(2,1)} %copy.101), channel_id=1, replica_groups=mesh['grp'=2,'freq'=16] {'freq'}, dimensions={2} | all-to-all | bytes 8388608 | tf_op jit(solution)/shard_map/all_to_all | solution.py:60
  544.6 4.3 fusion.73
  549.1 11.3 %multiply_reduce_fusion = (f32[]{:T(128)}, f32[]{:T(128)}, f32[256,8192]{1,0:T(8,128)}) fusion(s32[8192]{0:T(1024)S(1)} %bitcast.253, f32[]{:T(128)S(6)} %mul.210, f32[256,8192]{1,0:T(8,128)S(1)} %bitcast.229, f32[256,8192]{1,0:T(8,128)S(1)} %fusion.73, bf16[16,8,64,128]{3,2,1,0:T(8,128)(2,1)S(1)} %bitcast.245), kind=kOutput, calls=%fused_computation.53 | convolution fusion | flops 3240591360 | bytes 27295756 | tf_op jit(solution)/shard_map/dot_general | solution.py:40
  560.4 34.2 %all-reduce = (f32[]{:T(128)}, f32[]{:T(128)}, f32[]{:T(128)}) all-reduce(f32[]{:T(128)} %get-tuple-element.12, f32[]{:T(128)} %get-tuple-element.6, f32[]{:T(128)} %get-tuple-element.5), channel_id=1, replica_groups=mesh['grp'=2,'freq'=16] {'freq'}, use_global_device_ids=true, to_apply=%region_5.6 | all-reduce | flops 3 | bytes 24 | tf_op jit(solution)/shard_map/psum | solution.py:24
  596.6 7.1 divide_select_fusion
  603.8 5.8 fusion.93
  609.6 5.6 fusion.92
  619.1 4.8 all-to-all-start.3
  623.9 8.2 copy.144
  632.4 68.8 %all-to-all-done.3 = bf16[2,128,64,128]{3,2,0,1:T(8,128)(2,1)} async-done(((bf16[2,128,64,128]{3,2,0,1:T(8,128)(2,1)}), bf16[2,128,64,128]{3,2,0,1:T(8,128)(2,1)}, u32[]{:S(2)}, u32[]{:S(2)}) %all-to-all-start.3) | async-done | bytes 4194336 | tf_op jit(solution)/shard_map/all_to_all | solution.py:82
  701.2 3.1 copy.107
  706.8 14.0 %fusion.2 = f32[8,128,1024]{2,1,0:T(8,128)} fusion(bf16[8,1024,128]{2,1,0:T(8,128)(2,1)} %bitcast.243, bf16[2,8,1024,1024]{3,2,1,0:T(8,128)(2,1)} %param.3), kind=kOutput, calls=%fused_computation.2 | convolution fusion | flops 2147483648 | bytes 23068672 | tf_op jit(solution)/shard_map/ptx,pxi->pti/dot_general | solution.py:89
  722.4 14.3 %fusion = f32[8,128,1024]{2,1,0:T(8,128)} fusion(bf16[8,1024,128]{2,1,0:T(8,128)(2,1)} %bitcast.248, bf16[2,8,1024,1024]{3,2,1,0:T(8,128)(2,1)} %param.3), kind=kOutput, calls=%fused_computation | convolution fusion | flops 2147483648 | bytes 23068672 | tf_op jit(solution)/shard_map/ptx,pxi->pti/dot_general | solution.py:94
  736.8 10.7 %subtract_bitcast_fusion = f32[1,8,1024,128]{2,3,1,0:T(8,128)S(1)} fusion(f32[8,128,1024]{2,1,0:T(8,128)} %fusion.2, bf16[8,1024,128]{2,1,0:T(8,128)(2,1)} %bitcast.249, bf16[2,8,1024,1024]{3,2,1,0:T(8,128)(2,1)} %param.3), kind=kOutput, calls=%fused_computation.70 | convolution fusion | flops 2148532224 | bytes 27262976 | tf_op jit(solution)/shard_map/ptx,pxi->pti/dot_general | solution.py:87
  747.4 11.2 %add_bitcast_fusion = f32[1,8,1024,128]{2,3,1,0:T(8,128)} fusion(f32[8,128,1024]{2,1,0:T(8,128)} %fusion, bf16[8,1024,128]{2,1,0:T(8,128)(2,1)S(1)} %bitcast.244, bf16[2,8,1024,1024]{3,2,1,0:T(8,128)(2,1)} %param.3), kind=kOutput, calls=%fused_computation.69 | convolution fusion | flops 2148532224 | bytes 27262976 | tf_op jit(solution)/shard_map/ptx,pxi->pti/dot_general | solution.py:92
  758.6 6.3 fusion.40
  765.0 8.2 copy.149
  773.2 48.3 %psum.47 = f32[]{:T(128)} all-reduce(f32[]{:T(128)} %fusion.40), channel_id=1, replica_groups=mesh['grp'=2,'freq'=16] {'freq'}, use_global_device_ids=true, to_apply=%region_11.12 | all-reduce | flops 1 | bytes 8 | tf_op jit(solution)/shard_map/psum | solution.py:24
  822.4 9.7 %multiply_add_fusion = f32[256,64,128]{2,1,0:T(8,128)} fusion(f32[32,8,64,128]{3,2,1,0:T(8,128)} %copy.149, f32[32,8,64,128]{3,2,1,0:T(8,128)} %copy.144, f32[]{:T(128)S(6)} %div.94, f32[]{:T(128)S(6)} %sqrt.25, f32[]{:T(128)S(6)} %sqrt.23, f32[]{:T(128)S(6)} %div.89, f32[]{:T(128)S(6)} %mul.210, s32[64,128]{1,0:T(8,128)S(1)} %copy-done.4, f32[]{:T(128)S(6)} %div.77), kind=kLoop, calls=%fused_computation.51 | loop fusion | flops 27262976 | bytes 25198616 | tf_op jit(solution)/shard_map/add | solution.py:115
  (36 shorter events, 19.8 us)
Async XLA Ops:
  154.5 4.4 copy-start.4
  206.5 10.7 %copy-start = (f32[256,8192]{1,0:T(8,128)S(1)}, f32[256,8192]{1,0:T(8,128)}, u32[]{:S(2)}) copy-start(f32[256,8192]{1,0:T(8,128)} %get-tuple-element.25) | copy-start | bytes 25165828
  229.2 82.0 %all-to-all-start.1 = ((bf16[2,128,64,128]{3,2,0,1:T(8,128)(2,1)}), bf16[2,128,64,128]{3,2,0,1:T(8,128)(2,1)}, u32[]{:S(2)}, u32[]{:S(2)}) async-start(bf16[2,128,64,128]{3,2,0,1:T(8,128)(2,1)} %pad_maximum_fusion.1), calls=%async_computation.1 | async-start | bytes 8388608 | tf_op jit(solution)/shard_map/all_to_all | solution.py:82
  346.5 10.8 %copy-start.2 = (bf16[1,8,16,64,128]{4,3,2,1,0:T(8,128)(2,1)S(1)}, bf16[1,8,16,64,128]{4,3,2,1,0:T(8,128)(2,1)}, u32[]{:S(2)}) copy-start(bf16[1,8,16,64,128]{4,3,2,1,0:T(8,128)(2,1)} %copy.89) | copy-start | bytes 6291460
  374.9 3.2 copy-start.1
  543.4 5.7 slice-start
  544.6 4.5 slice-start.1
  619.1 82.0 %all-to-all-start.3 = ((bf16[2,128,64,128]{3,2,0,1:T(8,128)(2,1)}), bf16[2,128,64,128]{3,2,0,1:T(8,128)(2,1)}, u32[]{:S(2)}, u32[]{:S(2)}) async-start(bf16[2,128,64,128]{3,2,0,1:T(8,128)(2,1)} %pad_maximum_fusion.3), calls=%async_computation.3 | async-start | bytes 8388608 | tf_op jit(solution)/shard_map/all_to_all | solution.py:82
  736.7 10.7 %copy-start.3 = (bf16[1,8,16,64,128]{4,3,2,1,0:T(8,128)(2,1)S(1)}, bf16[1,8,16,64,128]{4,3,2,1,0:T(8,128)(2,1)}, u32[]{:S(2)}) copy-start(bf16[1,8,16,64,128]{4,3,2,1,0:T(8,128)(2,1)} %copy.111) | copy-start | bytes 6291460
where the time goes:
time: 836 us; the launch traced here: 832 us
  blocking collectives  328 us (39%)
  matrix products  244 us (29%)
  waiting for transfers between devices  138 us (17%)
  local copies, waits for them, and re-layouts  60.7 us (7%)
  other arithmetic  47.7 us (6%)
  starting transfers between devices  9.31 us (1%)
    all_to_all x2, blocking collectives, apply_adjoint(): lax.all_to_all(image, 'freq', split_axis=2, concat_axis=1, tiled=True)  211 us
    all_to_all x2, waiting for transfers between devices, body(): lax.all_to_all(spectrum, 'freq', split_axis=1, concat_axis=2, tiled=True)  138 us
    psum x3, blocking collectives, joint_total(): return lax.psum((first, second, third), 'freq')  117 us
    unnamed x22, local copies, waits for them, and re-layouts  31.8 us
    dot_general x2, matrix products, body(): jnp.einsum('ptx,pxi->pti', kernel_imaginary, solution_real, preferred_ele...  28.3 us
    dot_general x2, matrix products, body(): jnp.einsum('ptx,pxi->pti', kernel_imaginary, solution_imaginary, preferre...  28 us
    dot_general x2, matrix products, invert(): jnp.dot(sin_tab.T, widened[1].reshape(NF, -1), precision=highest)  23.4 us
    dot_general x2, matrix products, body(): jnp.einsum('ptx,pxi->pti', kernel_real, solution_imaginary, preferred_ele...  22.4 us
  transfers between devices with their start and end apart: 2, of which 2 were waited for; matrix products, arithmetic and copies ran while one was open for 2% of the time, Pallas kernels for 0%

commit v1 on v0

--- a/solution.py
+++ b/solution.py
@@ -57,7 +57,14 @@
             "hvi,hvg->hig", kernel_imaginary, update_real, preferred_element_type=jnp.float32
         )
         image = jnp.stack([z_real, z_imag]).astype(jnp.bfloat16)
-        timed = invert(lax.all_to_all(image, "freq", split_axis=2, concat_axis=1, tiled=True))
+        timed = invert(
+            jnp.concatenate(
+                lax.all_to_all(
+                    jnp.stack(jnp.split(image, lax.axis_size("freq"), axis=2)), "freq", 0, 0
+                ),
+                axis=1,
+            )
+        )
         return timed * keep_mask
 
     model_raw = apply_adjoint(recorded)

time: 836 us -> 845 us (1.011)
  other arithmetic: 47.7 us -> 60.1 us
    unnamed x1 -> x31, other arithmetic: 0.01 us -> 15.6 us
    unnamed x22 -> x27, local copies, waits for them, and re-layouts: 31.8 us -> 33.5 us
where the time goes in v1:
time: 845 us; the launch traced here: 842 us
  blocking collectives  328 us (39%)
  matrix products  244 us (29%)
  waiting for transfers between devices  137 us (16%)
  other arithmetic  60.1 us (7%)
  local copies, waits for them, and re-layouts  57.8 us (7%)
  starting transfers between devices  9.5 us (1%)
    all_to_all x2, blocking collectives, apply_adjoint(): lax.all_to_all(jnp.stack(jnp.split(image, lax.axis_size('freq'), axis=2))...  211 us
    all_to_all x2, waiting for transfers between devices, body(): lax.all_to_all(spectrum, 'freq', split_axis=1, concat_axis=2, tiled=True)  137 us
    psum x3, blocking collectives, joint_total(): return lax.psum((first, second, third), 'freq')  117 us
    unnamed x27, local copies, waits for them, and re-layouts  33.5 us
    dot_general x2, matrix products, body(): jnp.einsum('ptx,pxi->pti', kernel_imaginary, solution_real, preferred_ele...  28.3 us
    dot_general x2, matrix products, body(): jnp.einsum('ptx,pxi->pti', kernel_imaginary, solution_imaginary, preferre...  28.1 us
    dot_general x2, matrix products, invert(): jnp.dot(sin_tab.T, widened[1].reshape(NF, -1), precision=highest)  23.4 us
    dot_general x2, matrix products, apply_adjoint(): jnp.einsum('hvi,hvg->hig', kernel_imaginary, update_imaginary, preferred_...  22.4 us
  transfers between devices with their start and end apart: 2, of which 2 were waited for; matrix products, arithmetic and copies ran while one was open for 2% of the time, Pallas kernels for 0%

profile of v1, /device:TPU:0, one launch (start us, length us, event | category | flops | bytes accessed | tf_op | source)
XLA Modules:
  0.0 841.9 jit_solution(9579811482465128814)
XLA Ops:
  0.0 8.5 %multiply_reduce_fusion.3 = (f32[]{:T(128)}, bf16[2,8,1024,128]{3,2,1,0:T(8,128)(2,1)S(1)}) fusion(f32[2,8,1024,128]{3,2,1,0:T(8,128)} %param.4), kind=kLoop, calls=%fused_computation.117 | loop fusion | flops 6291455 | bytes 12582916 | tf_op jit(solution)/shard_map/reduce_sum | solution.py:20
  8.5 10.8 %fusion.14 = f32[8,1024,128]{2,1,0:T(8,128)} fusion(bf16[2,8,1024,1024]{3,2,1,0:T(8,128)(2,1)} %param.3, bf16[2,8,1024,128]{3,2,1,0:T(8,128)(2,1)S(1)} %get-tuple-element.15), kind=kOutput, calls=%fused_computation.14 | convolution fusion | flops 2147483648 | bytes 23068672 | tf_op jit(solution)/shard_map/hvi,hvg->hig/dot_general | solution.py:51
  19.3 10.7 %fusion.12 = f32[8,1024,128]{2,1,0:T(8,128)} fusion(bf16[2,8,1024,1024]{3,2,1,0:T(8,128)(2,1)} %param.3, bf16[2,8,1024,128]{3,2,1,0:T(8,128)(2,1)S(1)} %get-tuple-element.15), kind=kOutput, calls=%fused_computation.12 | convolution fusion | flops 2147483648 | bytes 23068672 | tf_op jit(solution)/shard_map/hvi,hvg->hig/dot_general | solution.py:56
  30.0 9.6 %fusion.67 = bf16[1,8,1024,128]{3,2,1,0:T(8,128)(2,1)S(1)} fusion(f32[8,1024,128]{2,1,0:T(8,128)} %fusion.14, bf16[2,8,1024,128]{3,2,1,0:T(8,128)(2,1)S(1)} %get-tuple-element.15, bf16[2,8,1024,1024]{3,2,1,0:T(8,128)(2,1)} %param.3), kind=kOutput, calls=%fused_computation.154 | convolution fusion | flops 2149580800 | bytes 25165824 | tf_op jit(solution)/shard_map/hvi,hvg->hig/dot_general | solution.py:49
  39.7 10.2 %fusion.68 = bf16[1,8,1024,128]{3,2,1,0:T(8,128)(2,1)S(1)} fusion(f32[8,1024,128]{2,1,0:T(8,128)} %fusion.12, bf16[2,8,1024,128]{3,2,1,0:T(8,128)(2,1)S(1)} %get-tuple-element.15, bf16[2,8,1024,1024]{3,2,1,0:T(8,128)(2,1)} %param.3), kind=kOutput, calls=%fused_computation.155 | convolution fusion | flops 2149580800 | bytes 25165824 | tf_op jit(solution)/shard_map/hvi,hvg->hig/dot_general | solution.py:54
  50.6 99.3 %all_to_all.40 = bf16[16,2,8,64,128]{4,3,2,1,0:T(8,128)(2,1)S(1)} all-to-all(bf16[16,2,8,64,128]{4,3,2,1,0:T(8,128)(2,1)S(1)} %fusion.138), channel_id=1, replica_groups=mesh['grp'=2,'freq'=16] {'freq'}, dimensions={0} | all-to-all | bytes 8388608 | tf_op jit(solution)/shard_map/all_to_all | solution.py:62
  151.5 4.4 fusion.78
  155.9 12.1 %multiply_reduce_fusion.4 = (f32[]{:T(128)}, f32[256,8192]{1,0:T(8,128)}) fusion(s32[8192]{0:T(1024)S(1)} %bitcast.312, f32[256,8192]{1,0:T(8,128)S(1)} %fusion.78, bf16[16,8,64,128]{3,2,1,0:T(8,128)(2,1)S(1)} %get-tuple-element.22), kind=kOutput, calls=%fused_computation.118 | convolution fusion | flops 3232202752 | bytes 18907140 | tf_op jit(solution)/shard_map/dot_general | solution.py:40
  168.0 34.1 %all-reduce.1 = (f32[]{:T(128)}, f32[]{:T(128)}) all-reduce(f32[]{:T(128)} %get-tuple-element.24, f32[]{:T(128)} %get-tuple-element.14), channel_id=1, replica_groups=mesh['grp'=2,'freq'=16] {'freq'}, use_global_device_ids=true, to_apply=%region_1.2 | all-reduce | flops 2 | bytes 16 | tf_op jit(solution)/shard_map/psum | solution.py:24
  203.4 10.7 %fusion.89 = bf16[16,8,64,128]{3,1,2,0:T(8,128)(2,1)S(1)} fusion(s32[8192]{0:T(1024)S(1)} %bitcast.313, f32[256,8192]{1,0:T(8,128)} %get-tuple-element.25, f32[]{:T(128)S(6)} %mul.210), kind=kOutput, calls=%fused_computation.180 | convolution fusion | flops 3231154176 | bytes 10518532 | tf_op jit(solution)/shard_map/dot_general | solution.py:82
  214.1 7.2 fusion.94
  223.5 2.3 pad_maximum_fusion
  225.9 4.5 all-to-all-start.1
  230.4 8.7 %copy.90 = f32[2,8,1024,128]{2,3,1,0:T(8,128)} copy(f32[2,8,1024,128]{3,2,1,0:T(8,128)} %param.4) | data formatting | bytes 16777216 | tf_op args[1]
  239.1 68.8 %all-to-all-done.1 = bf16[2,128,64,128]{3,2,0,1:T(8,128)(2,1)} async-done(((bf16[2,128,64,128]{3,2,0,1:T(8,128)(2,1)}), bf16[2,128,64,128]{3,2,0,1:T(8,128)(2,1)}, u32[]{:S(2)}, u32[]{:S(2)}) %all-to-all-start.1) | async-done | bytes 4194336 | tf_op jit(solution)/shard_map/all_to_all | solution.py:89
  307.9 3.1 copy.79
  313.6 14.0 %fusion.10 = f32[8,128,1024]{2,1,0:T(8,128)} fusion(bf16[8,1024,128]{2,1,0:T(8,128)(2,1)} %bitcast.304, bf16[2,8,1024,1024]{3,2,1,0:T(8,128)(2,1)} %param.3), kind=kOutput, calls=%fused_computation.10 | convolution fusion | flops 2147483648 | bytes 23068672 | tf_op jit(solution)/shard_map/ptx,pxi->pti/dot_general | solution.py:96
  329.1 14.0 %fusion.8 = f32[8,128,1024]{2,1,0:T(8,128)} fusion(bf16[8,1024,128]{2,1,0:T(8,128)(2,1)} %bitcast.308, bf16[2,8,1024,1024]{3,2,1,0:T(8,128)(2,1)} %param.3), kind=kOutput, calls=%fused_computation.8 | convolution fusion | flops 2147483648 | bytes 23068672 | tf_op jit(solution)/shard_map/ptx,pxi->pti/dot_general | solution.py:101
  343.2 11.1 %subtract_bitcast_fusion.1 = f32[1,8,1024,128]{2,3,1,0:T(8,128)S(1)} fusion(f32[8,128,1024]{2,1,0:T(8,128)} %fusion.10, bf16[8,1024,128]{2,1,0:T(8,128)(2,1)} %bitcast.309, bf16[2,8,1024,1024]{3,2,1,0:T(8,128)(2,1)} %param.3), kind=kOutput, calls=%fused_computation.131 | convolution fusion | flops 2148532224 | bytes 27262976 | tf_op jit(solution)/shard_map/ptx,pxi->pti/dot_general | solution.py:94
  354.3 11.2 %add_bitcast_fusion.1 = f32[1,8,1024,128]{2,3,1,0:T(8,128)} fusion(f32[8,128,1024]{2,1,0:T(8,128)} %fusion.8, bf16[8,1024,128]{2,1,0:T(8,128)(2,1)S(1)} %bitcast.305, bf16[2,8,1024,1024]{3,2,1,0:T(8,128)(2,1)} %param.3), kind=kOutput, calls=%fused_computation.130 | convolution fusion | flops 2148532224 | bytes 27262976 | tf_op jit(solution)/shard_map/ptx,pxi->pti/dot_general | solution.py:99
  365.5 6.4 multiply_reduce_fusion.2
  371.9 3.2 copy-done.1
  375.8 11.6 %fusion.6 = f32[8,128,1024]{2,1,0:T(8,128)} fusion(bf16[2,8,1024,1024]{3,2,1,0:T(8,128)(2,1)} %param.3, bf16[2,8,1024,128]{2,3,1,0:T(8,128)(2,1)S(1)} %convert_element_type.32), kind=kOutput, calls=%fused_computation.6 | convolution fusion | flops 2147483648 | bytes 23068672 | tf_op jit(solution)/shard_map/hvi,hvg->hig/dot_general | solution.py:51
  387.4 10.1 %fusion.4 = f32[8,128,1024]{2,1,0:T(8,128)} fusion(bf16[2,8,1024,1024]{3,2,1,0:T(8,128)(2,1)} %param.3, bf16[2,8,1024,128]{2,3,1,0:T(8,128)(2,1)S(1)} %convert_element_type.32), kind=kOutput, calls=%fused_computation.4 | convolution fusion | flops 2147483648 | bytes 23068672 | tf_op jit(solution)/shard_map/hvi,hvg->hig/dot_general | solution.py:56
  397.5 9.4 %fusion.69 = bf16[1,8,1024,128]{2,3,1,0:T(8,128)(2,1)S(1)} fusion(f32[8,128,1024]{2,1,0:T(8,128)} %fusion.6, bf16[2,8,1024,1024]{3,2,1,0:T(8,128)(2,1)} %param.3, bf16[2,8,1024,128]{2,3,1,0:T(8,128)(2,1)S(1)} %convert_element_type.32), kind=kOutput, calls=%fused_computation.156 | convolution fusion | flops 2149580800 | bytes 25165824 | tf_op jit(solution)/shard_map/hvi,hvg->hig/dot_general | solution.py:49
  407.0 10.0 %fusion.70 = bf16[1,8,1024,128]{2,3,1,0:T(8,128)(2,1)S(1)} fusion(f32[8,128,1024]{2,1,0:T(8,128)} %fusion.4, bf16[2,8,1024,1024]{3,2,1,0:T(8,128)(2,1)} %param.3, bf16[2,8,1024,128]{2,3,1,0:T(8,128)(2,1)} %copy-done.2), kind=kOutput, calls=%fused_computation.157 | convolution fusion | flops 2149580800 | bytes 25165824 | tf_op jit(solution)/shard_map/hvi,hvg->hig/dot_general | solution.py:54
  433.0 8.6 %copy.95 = bf16[16,2,8,64,128]{4,3,2,1,0:T(8,128)(2,1)} copy(bf16[16,2,8,64,128]{3,4,2,1,0:T(8,128)(2,1)} %fusion.121) | data formatting | bytes 8388608 | tf_op jit(solution)/shard_map/stack | solution.py:63
  441.6 111.7 %all_to_all.41 = bf16[16,2,8,64,128]{4,3,2,1,0:T(8,128)(2,1)S(1)} all-to-all(bf16[16,2,8,64,128]{4,3,2,1,0:T(8,128)(2,1)} %copy.95), channel_id=1, replica_groups=mesh['grp'=2,'freq'=16] {'freq'}, dimensions={0} | all-to-all | bytes 8388608 | tf_op jit(solution)/shard_map/all_to_all | solution.py:62
  554.4 4.3 fusion.73
  558.8 11.4 %multiply_reduce_fusion = (f32[]{:T(128)}, f32[]{:T(128)}, f32[256,8192]{1,0:T(8,128)}) fusion(s32[8192]{0:T(1024)S(1)} %bitcast.315, f32[]{:T(128)S(6)} %mul.210, f32[256,8192]{1,0:T(8,128)S(1)} %bitcast.294, f32[256,8192]{1,0:T(8,128)S(1)} %fusion.73, bf16[16,8,64,128]{3,2,1,0:T(8,128)(2,1)S(1)} %get-tuple-element.18), kind=kOutput, calls=%fused_computation.113 | convolution fusion | flops 3240591360 | bytes 27295756 | tf_op jit(solution)/shard_map/dot_general | solution.py:40
  570.1 34.3 %all-reduce = (f32[]{:T(128)}, f32[]{:T(128)}, f32[]{:T(128)}) all-reduce(f32[]{:T(128)} %get-tuple-element.12, f32[]{:T(128)} %get-tuple-element.6, f32[]{:T(128)} %get-tuple-element.5), channel_id=1, replica_groups=mesh['grp'=2,'freq'=16] {'freq'}, use_global_device_ids=true, to_apply=%region_5.6 | all-reduce | flops 3 | bytes 24 | tf_op jit(solution)/shard_map/psum | solution.py:24
  606.4 7.1 divide_select_fusion
  613.5 5.8 fusion.93
  619.3 5.6 fusion.92
  626.5 2.3 pad_maximum_fusion.1
  628.8 5.0 all-to-all-start.3
  633.8 8.2 copy.135
  642.3 68.6 %all-to-all-done.3 = bf16[2,128,64,128]{3,2,0,1:T(8,128)(2,1)} async-done(((bf16[2,128,64,128]{3,2,0,1:T(8,128)(2,1)}), bf16[2,128,64,128]{3,2,0,1:T(8,128)(2,1)}, u32[]{:S(2)}, u32[]{:S(2)}) %all-to-all-start.3) | async-done | bytes 4194336 | tf_op jit(solution)/shard_map/all_to_all | solution.py:89
  710.9 3.1 copy.98
  715.0 1.6 copy.102
  716.5 14.0 %fusion.2 = f32[8,128,1024]{2,1,0:T(8,128)} fusion(bf16[8,1024,128]{2,1,0:T(8,128)(2,1)} %bitcast.306, bf16[2,8,1024,1024]{3,2,1,0:T(8,128)(2,1)} %param.3), kind=kOutput, calls=%fused_computation.2 | convolution fusion | flops 2147483648 | bytes 23068672 | tf_op jit(solution)/shard_map/ptx,pxi->pti/dot_general | solution.py:96
  732.1 14.2 %fusion = f32[8,128,1024]{2,1,0:T(8,128)} fusion(bf16[8,1024,128]{2,1,0:T(8,128)(2,1)} %bitcast.310, bf16[2,8,1024,1024]{3,2,1,0:T(8,128)(2,1)} %param.3), kind=kOutput, calls=%fused_computation | convolution fusion | flops 2147483648 | bytes 23068672 | tf_op jit(solution)/shard_map/ptx,pxi->pti/dot_general | solution.py:101
  746.4 10.7 %subtract_bitcast_fusion = f32[1,8,1024,128]{2,3,1,0:T(8,128)S(1)} fusion(f32[8,128,1024]{2,1,0:T(8,128)} %fusion.2, bf16[8,1024,128]{2,1,0:T(8,128)(2,1)} %bitcast.311, bf16[2,8,1024,1024]{3,2,1,0:T(8,128)(2,1)} %param.3), kind=kOutput, calls=%fused_computation.127 | convolution fusion | flops 2148532224 | bytes 27262976 | tf_op jit(solution)/shard_map/ptx,pxi->pti/dot_general | solution.py:94
  757.1 11.2 %add_bitcast_fusion = f32[1,8,1024,128]{2,3,1,0:T(8,128)} fusion(f32[8,128,1024]{2,1,0:T(8,128)} %fusion, bf16[8,1024,128]{2,1,0:T(8,128)(2,1)S(1)} %bitcast.307, bf16[2,8,1024,1024]{3,2,1,0:T(8,128)(2,1)} %param.3), kind=kOutput, calls=%fused_computation.126 | convolution fusion | flops 2148532224 | bytes 27262976 | tf_op jit(solution)/shard_map/ptx,pxi->pti/dot_general | solution.py:99
  768.3 6.3 fusion.40
  774.6 8.2 copy.140
  782.8 48.3 %psum.47 = f32[]{:T(128)} all-reduce(f32[]{:T(128)} %fusion.40), channel_id=1, replica_groups=mesh['grp'=2,'freq'=16] {'freq'}, use_global_device_ids=true, to_apply=%region_11.12 | all-reduce | flops 1 | bytes 8 | tf_op jit(solution)/shard_map/psum | solution.py:24
  832.0 9.7 %multiply_add_fusion = f32[256,64,128]{2,1,0:T(8,128)} fusion(f32[32,8,64,128]{3,2,1,0:T(8,128)} %copy.140, f32[32,8,64,128]{3,2,1,0:T(8,128)} %copy.135, f32[]{:T(128)S(6)} %div.94, f32[]{:T(128)S(6)} %sqrt.25, f32[]{:T(128)S(6)} %sqrt.23, f32[]{:T(128)S(6)} %div.89, f32[]{:T(128)S(6)} %mul.210, s32[64,128]{1,0:T(8,128)S(1)} %copy-done.6, f32[]{:T(128)S(6)} %div.77), kind=kLoop, calls=%fused_computation.111 | loop fusion | flops 27262976 | bytes 25198616 | tf_op jit(solution)/shard_map/add | solution.py:122
  (65 shorter events, 30.3 us)
Async XLA Ops:
  151.4 4.4 copy-start.5
  203.4 10.7 %copy-start = (f32[256,8192]{1,0:T(8,128)S(1)}, f32[256,8192]{1,0:T(8,128)}, u32[]{:S(2)}) copy-start(f32[256,8192]{1,0:T(8,128)} %get-tuple-element.25) | copy-start | bytes 25165828
  225.9 82.0 %all-to-all-start.1 = ((bf16[2,128,64,128]{3,2,0,1:T(8,128)(2,1)}), bf16[2,128,64,128]{3,2,0,1:T(8,128)(2,1)}, u32[]{:S(2)}, u32[]{:S(2)}) async-start(bf16[2,128,64,128]{3,2,0,1:T(8,128)(2,1)} %pad_maximum_fusion), calls=%async_computation.1 | async-start | bytes 8388608 | tf_op jit(solution)/shard_map/all_to_all | solution.py:89
  343.2 11.1 %copy-start.3 = (bf16[1,8,16,64,128]{4,3,2,1,0:T(8,128)(2,1)S(1)}, bf16[1,8,16,64,128]{4,3,2,1,0:T(8,128)(2,1)}, u32[]{:S(2)}) copy-start(bf16[1,8,16,64,128]{4,3,2,1,0:T(8,128)(2,1)} %copy.83) | copy-start | bytes 6291460
  371.9 3.2 copy-start.1
  375.8 21.7 %copy-start.2 = (bf16[2,8,1024,128]{2,3,1,0:T(8,128)(2,1)}, bf16[2,8,1024,128]{2,3,1,0:T(8,128)(2,1)S(1)}, u32[]{:S(2)}) copy-start(bf16[2,8,1024,128]{2,3,1,0:T(8,128)(2,1)S(1)} %convert_element_type.32) | copy-start | bytes 12582916
  553.3 5.4 slice-start
  554.4 4.3 slice-start.1
  554.4 4.3 copy-start.6
  628.8 82.0 %all-to-all-start.3 = ((bf16[2,128,64,128]{3,2,0,1:T(8,128)(2,1)}), bf16[2,128,64,128]{3,2,0,1:T(8,128)(2,1)}, u32[]{:S(2)}, u32[]{:S(2)}) async-start(bf16[2,128,64,128]{3,2,0,1:T(8,128)(2,1)} %pad_maximum_fusion.1), calls=%async_computation.3 | async-start | bytes 8388608 | tf_op jit(solution)/shard_map/all_to_all | solution.py:89
  746.4 10.7 %copy-start.4 = (bf16[1,8,16,64,128]{4,3,2,1,0:T(8,128)(2,1)S(1)}, bf16[1,8,16,64,128]{4,3,2,1,0:T(8,128)(2,1)}, u32[]{:S(2)}) copy-start(bf16[1,8,16,64,128]{4,3,2,1,0:T(8,128)(2,1)} %copy.102) | copy-start | bytes 6291460
